TPU v7x, 32 devices: a whole 2x2x4 slice. The times are simulated.
32 devices in a mesh: task: 4 (over y, x), tok: 8 (over z, core).
Axes of the slice: x: 2, y: 2, z: 4, core: 2. Of those that a mesh axis runs over, the one named last changes fastest.
Arguments:
- hidden: bfloat16 [4, 256, 3584], P('task', 'tok'), may hold values from -6 to 6
- attn_out: bfloat16 [4, 256, 3584], P('task', 'tok'), may hold values from -6 to 6
- gain_attn: bfloat16 [3584], replicated, may hold values from 0.5 to 1.5
- gain_mlp: bfloat16 [3584], replicated, may hold values from 0.5 to 1.5
- lengths: int32 [4, 2], P('task'), may hold values from 32 to 128
Outputs:
- gram_attn: float32 [8, 896, 1792], P('tok', 'task')
- gram_mlp: float32 [8, 896, 1792], P('tok', 'task')
All inputs are finite; a program needn't handle non-finite values.
Results may differ from a plain program's by a relative error of at most 0.0044.
Values may be sent and summed in bfloat16 or wider, within the bound.
A program may use at most 64 MiB of HBM per device.

v0:
```python
import functools

import jax
import jax.numpy as jnp
from jax import lax
from jax.experimental import pallas as pl
from jax.experimental.pallas import tpu as pltpu
from jax.sharding import PartitionSpec as P

LANES = 128
LENT = (2, 3)


def planes_in_product_order():
    plane = lax.axis_index("tok") // 2
    inner = jnp.logical_or(plane == 1, plane == 2)
    plane_1 = plane + 1 - 2 * (plane % 2)
    plane_2 = jnp.where(plane // 2 == 1, plane - 2, plane + 2)
    plane_3 = 3 - plane
    return (
        jnp.where(inner, plane_1, plane), jnp.where(inner, plane, plane_1),
        jnp.where(inner, plane_3, plane_2), jnp.where(inner, plane_2, plane_3),
    )


def product(rows, held, plane, which, columns=slice(None)):
    n_task = lax.axis_size("task")
    left = rows[pl.ds(plane * n_task, n_task), which]
    right = held[which, pl.ds(plane * 2 * n_task, 2 * n_task), :, columns]
    depth = left.shape[0] * left.shape[1]
    return lax.dot_general(
        left.reshape(depth, left.shape[2]), right.reshape(depth, right.shape[2]),
        (((0,), (0,)), ((), ())), preferred_element_type=jnp.float32,
    )


def last_kernel(held, rows, total, out_attn, out_mlp, staged, sent):
    row_count, column_band = out_attn.shape[1], out_attn.shape[2]
    plane = planes_in_product_order()[3]
    factor = 1.0 / (lax.axis_size("tok") * held.shape[2])
    n_bands = sent.shape[1]
    width = column_band // n_bands
    writes = []
    for which, out in ((0, out_attn), (1, out_mlp)):
        for band in range(n_bands):
            span = slice(band * width, (band + 1) * width)
            piece = total[which, :, span] + product(rows, held, plane, which, span)
            staged[which, 0, :, span] = piece[:row_count] * factor
            write = pltpu.make_async_copy(
                staged.at[which, :, :, span], out.at[:, :, span], sent.at[which, band]
            )
            write.start()
            writes.append(write)
    for write in writes:
        write.wait()


def gather_kernel(
    hidden_hbm, attn_hbm, gain_attn_hbm, gain_mlp_hbm, lengths_hbm, held, rows, total,
    hidden, attn_out, gain_attn, gain_mlp, lengths, mine, lent,
    loaded, got, row_got, row_sent, z_sent, side_sent, pair_sent,
):
    task, tok = lax.axis_index("task"), lax.axis_index("tok")
    n_task = lax.axis_size("task")
    plane, core = tok // 2, tok % 2
    band = plane % 2
    tok_dev, column_band = held.shape[2], held.shape[3]
    n_planes = held.shape[1] // (2 * n_task)
    inner = jnp.logical_or(plane == 1, plane == 2)
    outer = jnp.logical_not(inner)

    def flip(value, bit):
        return value + bit - 2 * bit * (value // bit % 2)

    task_x, task_y = flip(task, 1), flip(task, 2)
    task_d = flip(task_x, 2)
    plane_1, plane_2 = flip(plane, 1), flip(plane, 2)
    plane_3 = flip(plane_1, 2)
    near, far = jnp.where(inner, plane_3, plane_2), jnp.where(inner, plane_2, plane_3)
    order = (plane, plane_1, near, far)
    product_order = planes_in_product_order()

    def at(tasks, planes, cores):
        return {"task": tasks, "tok": planes * 2 + cores}

    def chunk(planes, tasks, cores):
        return planes * (2 * n_task) + tasks * 2 + cores

    own = chunk(plane, task, core)

    loads = [
        pltpu.make_async_copy(source, target, loaded.at[spot])
        for spot, (source, target) in enumerate((
            (hidden_hbm, hidden), (attn_hbm, attn_out), (gain_attn_hbm, gain_attn),
            (gain_mlp_hbm, gain_mlp), (lengths_hbm, lengths),
        ))
    ]
    for load in loads:
        load.start()
    peers = (
        at(task_x, plane, core), at(task_y, plane, core), at(task, plane, 1 - core),
        at(task, plane_1, core), at(task, plane_2, core), at(task, plane_3, core),
    )
    barrier = pltpu.get_barrier_semaphore()
    for peer in peers:
        pl.semaphore_signal(
            barrier, inc=1, device_id=peer, device_id_type=pl.DeviceIdType.MESH
        )
    for load in loads:
        load.wait()

    slab = 16
    seq_count = lengths.shape[1]
    seq_slots = tok_dev * lax.axis_size("tok") // seq_count
    for low in range(0, tok_dev, slab):
        part = pl.ds(low, slab)
        place = tok * tok_dev + low + lax.broadcasted_iota(jnp.int32, (slab, 1), 0)
        live = jnp.zeros((slab, 1), jnp.float32)
        for seq in range(seq_count):
            offset = place - seq * seq_slots
            inside = (offset >= 0) & (offset < seq_slots) & (offset < lengths[0, seq])
            live = jnp.where(inside, 1.0, live)
        first = hidden[0, part, :].astype(jnp.float32)
        mixed = first + attn_out[0, part, :].astype(jnp.float32)
        for which, values, gain in ((0, first, gain_attn), (1, mixed, gain_mlp)):
            done = (normed(values, gain[...].reshape(1, -1)) * live).astype(jnp.bfloat16)
            for side in range(2):
                mine[which, side, part, :] = done[:, side * column_band : (side + 1) * column_band]
    for which in range(2):
        held[which, own] = mine[which, band]

    pl.semaphore_wait(barrier, len(peers))
    to_x, to_y, to_pair, to_1, to_2, to_3 = peers

    def copy(source, which, q, sent, peer):
        return pltpu.make_async_remote_copy(
            src_ref=source, dst_ref=held.at[which, q], send_sem=sent,
            recv_sem=got.at[which, q], device_id=peer,
            device_id_type=pl.DeviceIdType.MESH,
        )

    started = []

    def send(*arguments):
        out = copy(*arguments)
        out.start()
        started.append(out)

    def arrive(which, q):
        copy(held.at[which, q], which, q, pair_sent.at[which, q], to_pair).wait_recv()

    def to_inner(which):
        return copy(mine.at[which, 1 - band], which, own, z_sent.at[which, 2], to_3)

    def relay(which):
        q = chunk(plane_1, task, core)
        return copy(held.at[which, q], which, q, z_sent.at[which, 3], to_2)

    def own_step(step, which):
        q = chunk(order[step], task, core)
        if step:
            arrive(which, q)
            source = held.at[which, q]
        else:
            source = mine.at[which, band]
        if step == 1:
            @pl.when(inner)
            def _():
                relay(which).start()
        send(source, which, q, side_sent.at[0, which, step], to_x)
        send(source, which, q, side_sent.at[1, which, step], to_y)
        if step == 0:
            @pl.when(inner)
            def _():
                to_inner(which).start()
            send(mine.at[which, 1 - band], which, own, z_sent.at[which, 0], to_1)
            send(source, which, own, z_sent.at[which, 1], to_2)
        send(source, which, q, pair_sent.at[which, q], to_pair)

    def side_step(step, which):
        for tasks, relayed, axis, peer in (
            (task_x, 0, 1, to_y), (task_y, 1, 0, to_x)
        ):
            q = chunk(order[step], tasks, core)
            arrive(which, q)
            if which == relayed:
                send(
                    held.at[which, q], which, q,
                    side_sent.at[axis, which, n_planes + step], peer,
                )
            send(held.at[which, q], which, q, pair_sent.at[which, q], to_pair)

    def diagonal_step(step, which):
        q = chunk(order[step], task_d, core)
        arrive(which, q)
        send(held.at[which, q], which, q, pair_sent.at[which, q], to_pair)

    row_count = column_band // 2 // n_task
    padded = rows.shape[3]
    window = min(padded + LANES, column_band)
    row_start = core * (column_band // 2) + task * row_count
    base = jnp.minimum(row_start // LANES * LANES, column_band - window)
    shift = window - (row_start - base)

    def row_copy(group):
        return pltpu.make_async_remote_copy(
            src_ref=rows.at[group], dst_ref=rows.at[group], send_sem=row_sent.at[group],
            recv_sem=row_got.at[group], device_id=to_1,
            device_id_type=pl.DeviceIdType.MESH,
        )

    everyone = (task, task_x, task_y, task_d)
    lends = [(1, member) for member in range(4)] + [(0, member) for member in LENT]
    gives = [
        (step, member) for step in range(n_planes - 1) for member in range(4)
        if step < 2 or (0, member) not in lends
    ]

    def lend_copy(step, tasks):
        group = order[step] * n_task + tasks
        return pltpu.make_async_remote_copy(
            src_ref=lent.at[step, tasks], dst_ref=rows.at[group], send_sem=row_sent.at[group],
            recv_sem=row_got.at[group], device_id=to_3,
            device_id_type=pl.DeviceIdType.MESH,
        )

    def rows_of(step, member):
        tasks = everyone[member]
        for which in range(2):
            arrive(which, chunk(order[step], tasks, 1 - core))
        group = order[step] * n_task + tasks

        def cut_into(target):
            for which in range(2):
                span = held[
                    which, pl.ds(group * 2, 2), :, pl.ds(pl.multiple_of(base, LANES), window)
                ]
                span = span.reshape(2 * tok_dev, window).astype(jnp.float32)
                span = pltpu.roll(span, shift, 1)
                target[which] = span[:, :padded].astype(jnp.bfloat16)

        @pl.when(outer)
        def _():
            cut_into(rows.at[group])

        if (step, member) in lends:
            @pl.when(inner)
            def _():
                cut_into(lent.at[step, tasks])

        return step, member, group

    def send_rows(waiting):
        step, member, group = waiting
        if (step, member) in gives:
            @pl.when(outer)
            def _():
                row_copy(group).start()

        if (step, member) in lends:
            @pl.when(inner)
            def _():
                lend_copy(step, everyone[member]).start()

    def cut(step, members):
        waiting = None
        for member in members:
            group = rows_of(step, member)
            if waiting is not None:
                send_rows(waiting)
            waiting = group
        return waiting

    def rows_arrive(step):
        @pl.when(inner)
        def _():
            for tasks in range(n_task):
                row_copy(product_order[step] * n_task + tasks).wait_recv()

    def multiply(step):
        rows_arrive(step)

        @pl.loop(0, 2)
        def _(which):
            piece = product(rows, held, product_order[step], which)
            if step == 0:
                total[which] = piece
            else:
                total[which] += piece

    every, sides = range(4), range(3)
    for which in range(2):
        own_step(0, which)
    for which in range(2):
        side_step(0, which)
        own_step(1, which)
    for which in range(2):
        side_step(1, which)
        own_step(2, which)
        diagonal_step(0, which)
    waiting = cut(0, every)
    for which in range(2):
        side_step(2, which)
        if which == 0:
            send_rows(waiting)
        own_step(3, which)
        diagonal_step(1, which)
    waiting = cut(1, every)
    for which in range(2):
        side_step(3, which)
        if which == 0:
            send_rows(waiting)
        diagonal_step(2, which)
    waiting = cut(2, every)
    multiply(0)
    send_rows(waiting)
    waiting = cut(3, sides)
    multiply(1)
    send_rows(waiting)
    for which in range(2):
        diagonal_step(3, which)
    multiply(2)
    cut(3, (3,))
    rows_arrive(3)

    for out in started:
        out.wait_send()

    @pl.when(inner)
    def _():
        for which in range(2):
            to_inner(which).wait_send()
            relay(which).wait_send()
        for step, member in lends:
            lend_copy(step, everyone[member]).wait_send()

    @pl.when(outer)
    def _():
        for step, member in gives:
            row_copy(order[step] * n_task + everyone[member]).wait_send()


def gathered(hidden, attn_out, gain_attn, gain_mlp, lengths):
    _, tok_dev, width = hidden.shape
    n_tok, n_task = lax.axis_size("tok"), lax.axis_size("task")
    column_band = width // 2
    row_count = column_band // 2 // n_task
    padded = -(-row_count // LANES) * LANES
    devices = n_tok * n_task
    groups = devices // 2
    vmem, hbm = (pl.BlockSpec(memory_space=space) for space in (pltpu.VMEM, pltpu.HBM))
    semaphores = pltpu.SemaphoreType.DMA
    held, rows, total = pl.pallas_call(
        gather_kernel,
        out_shape=(
            jax.ShapeDtypeStruct((2, devices, tok_dev, column_band), jnp.bfloat16),
            jax.ShapeDtypeStruct((groups, 2, 2 * tok_dev, padded), jnp.bfloat16),
            jax.ShapeDtypeStruct((2, padded, column_band), jnp.float32),
        ),
        in_specs=[hbm] * 5,
        out_specs=(vmem,) * 3,
        scratch_shapes=[
            pltpu.VMEM(hidden.shape, jnp.bfloat16),
            pltpu.VMEM(attn_out.shape, jnp.bfloat16),
            pltpu.VMEM(gain_attn.shape, jnp.bfloat16),
            pltpu.VMEM(gain_mlp.shape, jnp.bfloat16),
            pltpu.SMEM(lengths.shape, jnp.int32),
            pltpu.VMEM((2, 2, tok_dev, column_band), jnp.bfloat16),
            pltpu.VMEM((2, n_task, 2, 2 * tok_dev, padded), jnp.bfloat16),
            semaphores((5,)),
            semaphores((2, devices)),
            semaphores((groups,)),
            semaphores((groups,)),
            semaphores((2, 4)),
            semaphores((2, 2, n_tok)),
            semaphores((2, devices)),
        ],
        compiler_params=pltpu.CompilerParams(
            collective_id=0, has_side_effects=True, vmem_limit_bytes=24 * 2**20
        ),
    )(*(
        pltpu.with_memory_space_constraint(array, pltpu.HBM)
        for array in (hidden, attn_out, gain_attn, gain_mlp, lengths)
    ))
    shape = (1, row_count, column_band)
    n_bands = 2
    return pl.pallas_call(
        last_kernel,
        out_shape=(jax.ShapeDtypeStruct(shape, jnp.float32),) * 2,
        in_specs=[vmem] * 3,
        out_specs=(hbm, hbm),
        scratch_shapes=[
            pltpu.VMEM((2,) + shape, jnp.float32),
            semaphores((2, n_bands)),
        ],
        compiler_params=pltpu.CompilerParams(vmem_limit_bytes=12 * 2**20),
    )(held, rows, total)


def from_partner(block, axis, distance):
    count = lax.axis_size(axis)
    route = []
    for low in range(count):
        high = low | 1 << distance
        if high != low and high < count:
            route += [(low, high), (high, low)]
    return lax.ppermute(block, axis, route)


def normed(values, gain):
    scale = lax.rsqrt(jnp.mean(values * values, axis=-1, keepdims=True) + 1e-06)
    return values * scale * gain.astype(jnp.float32)


def per_device(hidden, attn_out, gain_attn, gain_mlp, lengths):
    tok_dev = hidden.shape[1]
    width = hidden.shape[2]
    n_tok = lax.axis_size("tok")
    n_task = lax.axis_size("task")
    block_side = min(4, max(2, n_tok // 16))
    token_parts = n_tok // (block_side * block_side)
    if (n_task, n_tok, block_side) == (4, 8, 2) and width % (4 * LANES) == 0 and tok_dev % 16 == 0:
        return gathered(hidden, attn_out, gain_attn, gain_mlp, lengths)
    column_band = width // block_side
    tile_rows = column_band // token_parts
    slice_rows = tok_dev // token_parts
    seq_count = lengths.shape[1]
    seq_slots = tok_dev * n_tok // seq_count
    place = lax.axis_index("tok") * tok_dev + jnp.arange(tok_dev, dtype=jnp.int32)
    which = place // seq_slots
    offset = place % seq_slots
    owner = which[:, None] == jnp.arange(seq_count, dtype=jnp.int32)[None, :]
    limit = jnp.sum(jnp.where(owner, lengths[0][None, :], 0), axis=1)
    live = (offset < limit).astype(jnp.float32)[:, None]
    first = hidden[0].astype(jnp.float32)
    x_attn = (normed(first, gain_attn) * live).astype(jnp.bfloat16)
    mixed = first + attn_out[0].astype(jnp.float32)
    x_mlp = (normed(mixed, gain_mlp) * live).astype(jnp.bfloat16)

    def bands(values):
        split = values.reshape(token_parts, slice_rows, block_side, column_band).transpose(
            2, 0, 1, 3
        )
        shape = (block_side, block_side, token_parts, slice_rows, column_band)
        left_side = jnp.broadcast_to(split[:, None], shape).reshape(n_tok, slice_rows, column_band)
        right_side = jnp.broadcast_to(split[None], shape).reshape(n_tok, slice_rows, column_band)
        return (left_side, right_side)

    left_attn, right_attn = bands(x_attn)
    left_mlp, right_mlp = bands(x_mlp)
    arrived = (
        lax.all_to_all(left_attn, "tok", split_axis=0, concat_axis=0, tiled=True),
        lax.all_to_all(right_attn, "tok", split_axis=0, concat_axis=0, tiled=True),
        lax.all_to_all(left_mlp, "tok", split_axis=0, concat_axis=0, tiled=True),
        lax.all_to_all(right_mlp, "tok", split_axis=0, concat_axis=0, tiled=True),
    )
    contract = (((0, 1), (0, 1)), ((), ()))
    tile_attn = lax.dot_general(
        arrived[0], arrived[1], contract, preferred_element_type=jnp.float32
    )
    tile_mlp = lax.dot_general(arrived[2], arrived[3], contract, preferred_element_type=jnp.float32)
    grams = (
        tile_attn.reshape(token_parts, tile_rows, column_band),
        tile_mlp.reshape(token_parts, tile_rows, column_band),
    )
    part_index = lax.axis_index("tok") % token_parts
    depth_bits = token_parts.bit_length() - 1

    def halve(current, bit):
        upper_bit = part_index // (1 << bit) % 2 == 1
        middle = current[0].shape[0] // 2
        outgoing = tuple(
            (jnp.where(upper_bit, piece[:middle], piece[middle:]) for piece in current)
        )
        kept = tuple((jnp.where(upper_bit, piece[middle:], piece[:middle]) for piece in current))
        incoming = from_partner(outgoing, "tok", bit)
        return tuple((mine + theirs for mine, theirs in zip(kept, incoming)))

    for bit in range(depth_bits - 1, -1, -1):
        grams = halve(grams, bit)
    shaped = tuple((piece.reshape(n_task, tile_rows // n_task, column_band) for piece in grams))
    grams = lax.psum_scatter(shaped, "task", scatter_dimension=0, tiled=True)
    factor = 1.0 / (tok_dev * n_tok)
    final_attn = grams[0] * factor
    final_mlp = grams[1] * factor
    return (final_attn, final_mlp)


def solution(mesh):
    return jax.shard_map(
        per_device,
        mesh=mesh,
        in_specs=(P("task", "tok", None), P("task", "tok", None), P(), P(), P("task", None)),
        out_specs=(P("tok", "task", None), P("tok", "task", None)),
        check_vma=False,
    )
```

profile of v0, /device:TPU:0, one launch (start us, length us, event | category | flops | bytes accessed | tf_op | source)
XLA Modules:
  0.0 44.9 jit_solution(10321120256562448768)
XLA Ops:
  0.6 42.2 %shard_map.68 = (bf16[2,32,32,1792]{3,2,1,0:T(8,128)(2,1)S(1)}, bf16[16,2,64,256]{3,2,1,0:T(8,128)(2,1)S(1)}, f32[2,256,1792]{2,1,0:T(8,128)S(1)}) custom-call(bf16[1,32,3584]{2,1,0:T(8,128)(2,1)} %hidden_hbm.1, bf16[1,32,3584]{2,1,0:T(8,128)(2,1)} %attn_hbm.1, bf16[3584]{0:T(1024)(128)(2,1)} %gain_attn_hbm.1, bf16[3584]{0:T(1024)(128)(2,1)} %gain_mlp_hbm.1, ...), custom_call_target="tpu_custom_call" | custom-call | tf_op jit(solution)/shard_map/pallas_call | solution.py:353
  42.8 2.1 %shard_map.69 = (f32[1,224,1792]{2,1,0:T(8,128)}, f32[1,224,1792]{2,1,0:T(8,128)}) custom-call(bf16[2,32,32,1792]{3,2,1,0:T(8,128)(2,1)S(1)} %get-tuple-element.5.held, bf16[16,2,64,256]{3,2,1,0:T(8,128)(2,1)S(1)} %get-tuple-element.6.rows, f32[2,256,1792]{2,1,0:T(8,128)S(1)} %get-tuple-element.7.total), custom_call_target="tpu_custom_call" | custom-call | tf_op jit(solution)/shard_map/pallas_call | solution.py:387
where the time goes:
time: 45 us; the launch traced here: 44.9 us
  Pallas kernels  44.2 us (98%)
  between operations  0.64 us (1%)
    pallas_call x1, Pallas kernels, gathered(): pl.pallas_call(gather_kernel, out_shape=(jax.ShapeDtypeStruct((2, devices...  42.2 us
    pallas_call x1, Pallas kernels, gathered(): pl.pallas_call(last_kernel, out_shape=(jax.ShapeDtypeStruct(shape, jnp.fl...  2.05 us

commit v1 on v0

--- a/solution.py
+++ b/solution.py
@@ -57,8 +57,8 @@
 
 def gather_kernel(
     hidden_hbm, attn_hbm, gain_attn_hbm, gain_mlp_hbm, lengths_hbm, held, rows, total,
-    hidden, attn_out, gain_attn, gain_mlp, lengths, mine, lent,
-    loaded, got, row_got, row_sent, z_sent, side_sent, pair_sent,
+    hidden, attn_out, gain_attn, gain_mlp, lengths, mine, lent, passing, rising,
+    loaded, ready, z_got, pass_got, rise_got, first_got, second_got, diagonal_got, pair_got, row_got, sent, row_sent,
 ):
     task, tok = lax.axis_index("task"), lax.axis_index("tok")
     n_task = lax.axis_size("task")
@@ -87,6 +87,8 @@
         return planes * (2 * n_task) + tasks * 2 + cores
 
     own = chunk(plane, task, core)
+    to_x, to_y, to_pair = at(task_x, plane, core), at(task_y, plane, core), at(task, plane, 1 - core)
+    to_1, to_2, to_3 = at(task, plane_1, core), at(task, plane_2, core), at(task, plane_3, core)
 
     loads = [
         pltpu.make_async_copy(source, target, loaded.at[spot])
@@ -97,17 +99,33 @@
     ]
     for load in loads:
         load.start()
-    peers = (
-        at(task_x, plane, core), at(task_y, plane, core), at(task, plane, 1 - core),
-        at(task, plane_1, core), at(task, plane_2, core), at(task, plane_3, core),
-    )
+
     barrier = pltpu.get_barrier_semaphore()
-    for peer in peers:
+    always, odd = plane >= 0, plane % 2 == 1
+    z_peers = (
+        (to_1, plane_1, always, always), (to_2, plane_2, always, odd),
+        (to_3, plane_3, inner, inner),
+    )
+
+    def signal(semaphore, peer):
         pl.semaphore_signal(
-            barrier, inc=1, device_id=peer, device_id_type=pl.DeviceIdType.MESH
+            semaphore, inc=1, device_id=peer, device_id_type=pl.DeviceIdType.MESH
         )
+
+    for peer in (to_x, to_y, to_pair):
+        signal(barrier, peer)
+    for peer, planes, met, _ in z_peers:
+        @pl.when(jnp.logical_and(met, planes > plane))
+        def _(peer=peer):
+            signal(barrier, peer)
+
     for load in loads:
         load.wait()
+    pl.semaphore_wait(barrier, 3 + jnp.minimum(plane, 2))
+    for reach, (peer, planes, _, answer) in enumerate(z_peers):
+        @pl.when(jnp.logical_and(answer, planes < plane))
+        def _(reach=reach, peer=peer):
+            signal(ready.at[reach], peer)
 
     slab = 16
     seq_count = lengths.shape[1]
@@ -129,71 +147,137 @@
     for which in range(2):
         held[which, own] = mine[which, band]
 
-    pl.semaphore_wait(barrier, len(peers))
-    to_x, to_y, to_pair, to_1, to_2, to_3 = peers
-
-    def copy(source, which, q, sent, peer):
+    def copy(source, which, q, got, peer):
         return pltpu.make_async_remote_copy(
-            src_ref=source, dst_ref=held.at[which, q], send_sem=sent,
-            recv_sem=got.at[which, q], device_id=peer,
+            src_ref=source, dst_ref=held.at[which, q], send_sem=sent.at[0],
+            recv_sem=got, device_id=peer, device_id_type=pl.DeviceIdType.MESH,
+        )
+
+    def send(*arguments):
+        copy(*arguments).start()
+
+    def arrived(span, got):
+        pltpu.make_async_remote_copy(
+            src_ref=span, dst_ref=span, send_sem=sent.at[0], recv_sem=got,
+            device_id=to_pair, device_id_type=pl.DeviceIdType.MESH,
+        ).wait_recv()
+
+    def pair_copy(step, member, which, q, source):
+        spot = step if step < n_planes - 1 else n_planes - 1 + member // 3
+        send(source, which, q, pair_got.at[spot], to_pair)
+
+    def own_step(step):
+        q = chunk(order[step], task, core)
+
+        def source(which):
+            return held.at[which, q] if step else mine.at[which, band]
+
+        def landed(which):
+            if step:
+                arrived(held.at[which, q], z_got.at[which, step - 1])
+
+        landed(0)
+        send(source(0), 0, q, first_got.at[0, step], to_x)
+        pair_copy(step, 0, 0, q, source(0))
+        landed(1)
+        send(source(1), 1, q, first_got.at[1, step], to_y)
+        send(source(1), 1, q, second_got.at[step], to_x)
+        send(source(0), 0, q, second_got.at[step], to_y)
+        pair_copy(step, 0, 1, q, source(1))
+
+    def answered(reach):
+        _, planes, met, answer = z_peers[reach]
+
+        @pl.when(jnp.logical_and(answer, planes > plane))
+        def _():
+            pl.semaphore_wait(ready.at[reach], 1)
+
+    def inward(planes):
+        @pl.when(plane == planes)
+        def _():
+            for which in range(2):
+                send(mine.at[which, 1 - band], which, own, z_got.at[which, 1], to_3)
+
+    def z_sends():
+        inward(2)
+        answered(0)
+        for which in range(2):
+            send(mine.at[which, 1 - band], which, own, z_got.at[which, 0], to_1)
+
+        @pl.when(outer)
+        def _():
+            for which in range(2):
+                outward(
+                    mine.at[which, band], passing.at[which], sent.at[0], pass_got.at[which], to_1
+                ).start()
+
+        answered(2)
+
+        @pl.when(plane == 1)
+        def _():
+            for which in range(2):
+                outward(
+                    mine.at[which, band], rising.at[which], sent.at[0], rise_got.at[which], to_3
+                ).start()
+
+        @pl.when(plane == 2)
+        def _():
+            for which in range(2):
+                send(mine.at[which, band], which, own, z_got.at[which, 1], to_2)
+
+    def outward(source, target, semaphore, got, peer):
+        return pltpu.make_async_remote_copy(
+            src_ref=source, dst_ref=target, send_sem=semaphore, recv_sem=got, device_id=peer,
             device_id_type=pl.DeviceIdType.MESH,
         )
 
-    started = []
-
-    def send(*arguments):
-        out = copy(*arguments)
-        out.start()
-        started.append(out)
-
-    def arrive(which, q):
-        copy(held.at[which, q], which, q, pair_sent.at[which, q], to_pair).wait_recv()
-
-    def to_inner(which):
-        return copy(mine.at[which, 1 - band], which, own, z_sent.at[which, 2], to_3)
-
-    def relay(which):
-        q = chunk(plane_1, task, core)
-        return copy(held.at[which, q], which, q, z_sent.at[which, 3], to_2)
-
-    def own_step(step, which):
-        q = chunk(order[step], task, core)
-        if step:
-            arrive(which, q)
-            source = held.at[which, q]
-        else:
-            source = mine.at[which, band]
-        if step == 1:
-            @pl.when(inner)
-            def _():
-                relay(which).start()
-        send(source, which, q, side_sent.at[0, which, step], to_x)
-        send(source, which, q, side_sent.at[1, which, step], to_y)
-        if step == 0:
-            @pl.when(inner)
-            def _():
-                to_inner(which).start()
-            send(mine.at[which, 1 - band], which, own, z_sent.at[which, 0], to_1)
-            send(source, which, own, z_sent.at[which, 1], to_2)
-        send(source, which, q, pair_sent.at[which, q], to_pair)
-
-    def side_step(step, which):
-        for tasks, relayed, axis, peer in (
-            (task_x, 0, 1, to_y), (task_y, 1, 0, to_x)
-        ):
+    def rise_on():
+        @pl.when(plane == 2)
+        def _():
+            q = chunk(plane_3, task, core)
+            for which in range(2):
+                arrived(rising.at[which], rise_got.at[which])
+                outward(
+                    rising.at[which], held.at[which, q], sent.at[2], z_got.at[which, 1], to_1
+                ).start()
+
+    def relay(planes):
+        @pl.when(plane == planes)
+        def _():
+            answered(1)
+            q = chunk(plane_1, task, core)
+            for which in range(2):
+                send(held.at[which, q], which, q, z_got.at[which, 2], to_2)
+
+    def pass_on():
+        @pl.when(inner)
+        def _():
+            q = chunk(plane_1, task, core)
+            for which in range(2):
+                arrived(passing.at[which], pass_got.at[which])
+                outward(
+                    passing.at[which], held.at[which, q], sent.at[1], z_got.at[which, 2], to_3
+                ).start()
+
+    def first_side(step):
+        for which, tasks, member, axis, peer in ((0, task_x, 1, 0, to_y), (1, task_y, 2, 1, to_x)):
             q = chunk(order[step], tasks, core)
-            arrive(which, q)
-            if which == relayed:
-                send(
-                    held.at[which, q], which, q,
-                    side_sent.at[axis, which, n_planes + step], peer,
-                )
-            send(held.at[which, q], which, q, pair_sent.at[which, q], to_pair)
-
-    def diagonal_step(step, which):
+            arrived(held.at[which, q], first_got.at[axis, step])
+            send(held.at[which, q], which, q, diagonal_got.at[step], peer)
+            pair_copy(step, member, which, q, held.at[which, q])
+
+    def second_side(step):
+        both = held.at[:, pl.ds(chunk(order[step], task_x, core), 1)]
+        arrived(both, second_got.at[step])
+        for which, tasks, member in ((1, task_x, 1), (0, task_y, 2)):
+            q = chunk(order[step], tasks, core)
+            pair_copy(step, member, which, q, held.at[which, q])
+
+    def diagonal_step(step):
         q = chunk(order[step], task_d, core)
-        arrive(which, q)
-        send(held.at[which, q], which, q, pair_sent.at[which, q], to_pair)
+        arrived(held.at[:, pl.ds(q, 1)], diagonal_got.at[step])
+        for which in range(2):
+            pair_copy(step, 3, which, q, held.at[which, q])
 
     row_count = column_band // 2 // n_task
     padded = rows.shape[3]
@@ -202,13 +286,6 @@
     base = jnp.minimum(row_start // LANES * LANES, column_band - window)
     shift = window - (row_start - base)
 
-    def row_copy(group):
-        return pltpu.make_async_remote_copy(
-            src_ref=rows.at[group], dst_ref=rows.at[group], send_sem=row_sent.at[group],
-            recv_sem=row_got.at[group], device_id=to_1,
-            device_id_type=pl.DeviceIdType.MESH,
-        )
-
     everyone = (task, task_x, task_y, task_d)
     lends = [(1, member) for member in range(4)] + [(0, member) for member in LENT]
     gives = [
@@ -216,66 +293,65 @@
         if step < 2 or (0, member) not in lends
     ]
 
-    def lend_copy(step, tasks):
-        group = order[step] * n_task + tasks
+    def row_copy(source, group, peer):
         return pltpu.make_async_remote_copy(
-            src_ref=lent.at[step, tasks], dst_ref=rows.at[group], send_sem=row_sent.at[group],
-            recv_sem=row_got.at[group], device_id=to_3,
+            src_ref=source, dst_ref=rows.at[group], send_sem=row_sent.at[0],
+            recv_sem=row_got.at[group // n_task], device_id=peer,
             device_id_type=pl.DeviceIdType.MESH,
         )
 
-    def rows_of(step, member):
-        tasks = everyone[member]
-        for which in range(2):
-            arrive(which, chunk(order[step], tasks, 1 - core))
-        group = order[step] * n_task + tasks
-
-        def cut_into(target):
-            for which in range(2):
-                span = held[
-                    which, pl.ds(group * 2, 2), :, pl.ds(pl.multiple_of(base, LANES), window)
-                ]
-                span = span.reshape(2 * tok_dev, window).astype(jnp.float32)
-                span = pltpu.roll(span, shift, 1)
-                target[which] = span[:, :padded].astype(jnp.bfloat16)
-
-        @pl.when(outer)
-        def _():
-            cut_into(rows.at[group])
-
-        if (step, member) in lends:
-            @pl.when(inner)
-            def _():
-                cut_into(lent.at[step, tasks])
-
-        return step, member, group
-
-    def send_rows(waiting):
-        step, member, group = waiting
-        if (step, member) in gives:
+    def cut(step, members):
+        low = chunk(order[step], 0, 0)
+        span = held.at[:, pl.ds(low, len(members))]
+        arrived(span, pair_got.at[step if step < n_planes - 1 else n_planes - 1 + members[0] // 3])
+        for member in members:
+            tasks = everyone[member]
+            group = order[step] * n_task + tasks
+
+            def cut_into(target, group=group):
+                for which in range(2):
+                    span = held[
+                        which, pl.ds(group * 2, 2), :, pl.ds(pl.multiple_of(base, LANES), window)
+                    ]
+                    span = span.reshape(2 * tok_dev, window).astype(jnp.float32)
+                    span = pltpu.roll(span, shift, 1)
+                    target[which] = span[:, :padded].astype(jnp.bfloat16)
+
             @pl.when(outer)
             def _():
-                row_copy(group).start()
-
-        if (step, member) in lends:
-            @pl.when(inner)
-            def _():
-                lend_copy(step, everyone[member]).start()
-
-    def cut(step, members):
-        waiting = None
-        for member in members:
-            group = rows_of(step, member)
-            if waiting is not None:
-                send_rows(waiting)
-            waiting = group
-        return waiting
+                cut_into(rows.at[group])
+
+            if (step, member) in lends:
+                @pl.when(inner)
+                def _():
+                    cut_into(lent.at[step, tasks])
+
+    def give_rows(step, members):
+        @pl.when(outer)
+        def _():
+            for member in members:
+                if (step, member) in gives:
+                    group = order[step] * n_task + everyone[member]
+                    row_copy(rows.at[group], group, to_1).start()
+
+    def lend_rows(step, members):
+        @pl.when(inner)
+        def _():
+            for member in members:
+                if (step, member) in lends:
+                    tasks = everyone[member]
+                    group = order[step] * n_task + tasks
+                    row_copy(lent.at[step, tasks], group, to_3).start()
 
     def rows_arrive(step):
         @pl.when(inner)
         def _():
-            for tasks in range(n_task):
-                row_copy(product_order[step] * n_task + tasks).wait_recv()
+            planes = product_order[step]
+            span = rows.at[pl.ds(planes * n_task, n_task)]
+            pltpu.make_async_remote_copy(
+                src_ref=span, dst_ref=span, send_sem=row_sent.at[0], recv_sem=row_got.at[planes],
+                device_id=to_1, device_id_type=pl.DeviceIdType.MESH,
+            ).wait_recv()
 
     def multiply(step):
         rows_arrive(step)
@@ -288,56 +364,65 @@
             else:
                 total[which] += piece
 
-    every, sides = range(4), range(3)
-    for which in range(2):
-        own_step(0, which)
-    for which in range(2):
-        side_step(0, which)
-        own_step(1, which)
-    for which in range(2):
-        side_step(1, which)
-        own_step(2, which)
-        diagonal_step(0, which)
-    waiting = cut(0, every)
-    for which in range(2):
-        side_step(2, which)
-        if which == 0:
-            send_rows(waiting)
-        own_step(3, which)
-        diagonal_step(1, which)
-    waiting = cut(1, every)
-    for which in range(2):
-        side_step(3, which)
-        if which == 0:
-            send_rows(waiting)
-        diagonal_step(2, which)
-    waiting = cut(2, every)
+    every = (0, 1, 2, 3)
+    own_step(0)
+    z_sends()
+    first_side(0)
+    own_step(1)
+    inward(1)
+    rise_on()
+    second_side(0)
+    diagonal_step(0)
+    relay(2)
+    first_side(1)
+    cut(0, every)
+    pass_on()
+    give_rows(0, every)
+    own_step(2)
+    second_side(1)
+    relay(1)
+    diagonal_step(1)
+    first_side(2)
+    own_step(3)
+    cut(1, every)
+    give_rows(1, every)
+    lend_rows(0, every)
+    second_side(2)
     multiply(0)
-    send_rows(waiting)
-    waiting = cut(3, sides)
+    diagonal_step(2)
+    lend_rows(1, every)
+    first_side(3)
+    cut(2, every)
+    give_rows(2, every)
     multiply(1)
-    send_rows(waiting)
-    for which in range(2):
-        diagonal_step(3, which)
+    second_side(3)
     multiply(2)
+    diagonal_step(3)
+    cut(3, (0, 1, 2))
     cut(3, (3,))
     rows_arrive(3)
 
-    for out in started:
-        out.wait_send()
+    def all_sent(span, semaphore):
+        pltpu.make_async_remote_copy(
+            src_ref=span, dst_ref=span, send_sem=semaphore, recv_sem=row_got.at[0],
+            device_id=to_pair, device_id_type=pl.DeviceIdType.MESH,
+        ).wait_send()
 
     @pl.when(inner)
     def _():
-        for which in range(2):
-            to_inner(which).wait_send()
-            relay(which).wait_send()
-        for step, member in lends:
-            lend_copy(step, everyone[member]).wait_send()
+        all_sent(held, sent.at[0])
+        all_sent(passing, sent.at[1])
+
+        @pl.when(plane == 2)
+        def _():
+            all_sent(rising, sent.at[2])
+
+        all_sent(rows.at[pl.ds(0, len(lends))], row_sent.at[0])
 
     @pl.when(outer)
     def _():
-        for step, member in gives:
-            row_copy(order[step] * n_task + everyone[member]).wait_send()
+        all_sent(held.at[:, pl.ds(0, held.shape[1] - 2)], sent.at[0])
+        all_sent(rows.at[pl.ds(0, len(gives))], row_sent.at[0])
 
 
 def gathered(hidden, attn_out, gain_attn, gain_mlp, lengths):
@@ -367,13 +452,20 @@
             pltpu.SMEM(lengths.shape, jnp.int32),
             pltpu.VMEM((2, 2, tok_dev, column_band), jnp.bfloat16),
             pltpu.VMEM((2, n_task, 2, 2 * tok_dev, padded), jnp.bfloat16),
+            pltpu.VMEM((2, tok_dev, column_band), jnp.bfloat16),
+            pltpu.VMEM((2, tok_dev, column_band), jnp.bfloat16),
             semaphores((5,)),
-            semaphores((2, devices)),
-            semaphores((groups,)),
-            semaphores((groups,)),
+            pltpu.SemaphoreType.REGULAR((3,)),
+            semaphores((2, 3)),
+            semaphores((2,)),
+            semaphores((2,)),
             semaphores((2, 4)),
-            semaphores((2, 2, n_tok)),
-            semaphores((2, devices)),
+            semaphores((4,)),
+            semaphores((4,)),
+            semaphores((5,)),
+            semaphores((4,)),
+            semaphores((3,)),
+            semaphores((1,)),
         ],
         compiler_params=pltpu.CompilerParams(
             collective_id=0, has_side_effects=True, vmem_limit_bytes=24 * 2**20

time: 45 us -> 41.7 us (0.927)
  the two profiles are of different devices: /device:TPU:0 before, /device:TPU:21 now
where the time goes in v1:
time: 41.7 us; the launch traced here: 41.6 us
  Pallas kernels  40.9 us (98%)
  between operations  0.64 us (2%)
    pallas_call x1, Pallas kernels, gathered(): pl.pallas_call(gather_kernel, out_shape=(jax.ShapeDtypeStruct((2, devices...  38.9 us
    pallas_call x1, Pallas kernels, gathered(): pl.pallas_call(last_kernel, out_shape=(jax.ShapeDtypeStruct(shape, jnp.fl...  2.05 us

profile of v1, /device:TPU:21, one launch (start us, length us, event | category | flops | bytes accessed | tf_op | source)
XLA Modules:
  0.0 41.6 jit_solution(13689669743659740321)
XLA Ops:
  0.6 38.9 %shard_map.68 = (bf16[2,32,32,1792]{3,2,1,0:T(8,128)(2,1)S(1)}, bf16[16,2,64,256]{3,2,1,0:T(8,128)(2,1)S(1)}, f32[2,256,1792]{2,1,0:T(8,128)S(1)}) custom-call(bf16[1,32,3584]{2,1,0:T(8,128)(2,1)} %hidden_hbm.1, bf16[1,32,3584]{2,1,0:T(8,128)(2,1)} %attn_hbm.1, bf16[3584]{0:T(1024)(128)(2,1)} %gain_attn_hbm.1, bf16[3584]{0:T(1024)(128)(2,1)} %gain_mlp_hbm.1, ...), custom_call_target="tpu_custom_call" | custom-call | tf_op jit(solution)/shard_map/pallas_call | solution.py:438
  39.5 2.1 %shard_map.69 = (f32[1,224,1792]{2,1,0:T(8,128)}, f32[1,224,1792]{2,1,0:T(8,128)}) custom-call(bf16[2,32,32,1792]{3,2,1,0:T(8,128)(2,1)S(1)} %get-tuple-element.5.held, bf16[16,2,64,256]{3,2,1,0:T(8,128)(2,1)S(1)} %get-tuple-element.6.rows, f32[2,256,1792]{2,1,0:T(8,128)S(1)} %get-tuple-element.7.total), custom_call_target="tpu_custom_call" | custom-call | tf_op jit(solution)/shard_map/pallas_call | solution.py:479

commit v2 on v1

--- a/solution.py
+++ b/solution.py
@@ -279,6 +279,11 @@
         for which in range(2):
             pair_copy(step, 3, which, q, held.at[which, q])
 
+    def diagonal_last(now):
+        @pl.when(now)
+        def _():
+            diagonal_step(n_planes - 1)
+
     row_count = column_band // 2 // n_task
     padded = rows.shape[3]
     window = min(padded + LANES, column_band)
@@ -375,17 +380,17 @@
     diagonal_step(0)
     relay(2)
     first_side(1)
+    pass_on()
     cut(0, every)
-    pass_on()
     give_rows(0, every)
     own_step(2)
     second_side(1)
     relay(1)
     diagonal_step(1)
     first_side(2)
-    own_step(3)
     cut(1, every)
     give_rows(1, every)
+    own_step(3)
     lend_rows(0, every)
     second_side(2)
     multiply(0)
@@ -396,8 +401,9 @@
     give_rows(2, every)
     multiply(1)
     second_side(3)
+    diagonal_last(inner)
     multiply(2)
-    diagonal_step(3)
+    diagonal_last(outer)
     cut(3, (0, 1, 2))
     cut(3, (3,))
     rows_arrive(3)
@@ -475,7 +481,7 @@
         for array in (hidden, attn_out, gain_attn, gain_mlp, lengths)
     ))
     shape = (1, row_count, column_band)
-    n_bands = 2
+    n_bands = column_band // (2 * LANES)
     return pl.pallas_call(
         last_kernel,
         out_shape=(jax.ShapeDtypeStruct(shape, jnp.float32),) * 2,

time: 41.7 us -> 39.4 us (0.945)
  the two profiles are of different devices: /device:TPU:21 before, /device:TPU:0 now
where the time goes in v2:
time: 39.4 us; the launch traced here: 39.3 us
  Pallas kernels  38.6 us (98%)
  between operations  0.64 us (2%)
    pallas_call x1, Pallas kernels, gathered(): pl.pallas_call(gather_kernel, out_shape=(jax.ShapeDtypeStruct((2, devices...  36.5 us
    pallas_call x1, Pallas kernels, gathered(): pl.pallas_call(last_kernel, out_shape=(jax.ShapeDtypeStruct(shape, jnp.fl...  2.1 us

profile of v2, /device:TPU:0, one launch (start us, length us, event | category | flops | bytes accessed | tf_op | source)
XLA Modules:
  0.0 39.3 jit_solution(77711461061812027)
XLA Ops:
  0.6 36.5 %shard_map.68 = (bf16[2,32,32,1792]{3,2,1,0:T(8,128)(2,1)S(1)}, bf16[16,2,64,256]{3,2,1,0:T(8,128)(2,1)S(1)}, f32[2,256,1792]{2,1,0:T(8,128)S(1)}) custom-call(bf16[1,32,3584]{2,1,0:T(8,128)(2,1)} %hidden_hbm.1, bf16[1,32,3584]{2,1,0:T(8,128)(2,1)} %attn_hbm.1, bf16[3584]{0:T(1024)(128)(2,1)} %gain_attn_hbm.1, bf16[3584]{0:T(1024)(128)(2,1)} %gain_mlp_hbm.1, ...), custom_call_target="tpu_custom_call" | custom-call | tf_op jit(solution)/shard_map/pallas_call | solution.py:444
  37.2 2.1 %shard_map.69 = (f32[1,224,1792]{2,1,0:T(8,128)}, f32[1,224,1792]{2,1,0:T(8,128)}) custom-call(bf16[2,32,32,1792]{3,2,1,0:T(8,128)(2,1)S(1)} %get-tuple-element.5.held, bf16[16,2,64,256]{3,2,1,0:T(8,128)(2,1)S(1)} %get-tuple-element.6.rows, f32[2,256,1792]{2,1,0:T(8,128)S(1)} %get-tuple-element.7.total), custom_call_target="tpu_custom_call" | custom-call | tf_op jit(solution)/shard_map/pallas_call | solution.py:485

commit v3 on v2

--- a/solution.py
+++ b/solution.py
@@ -23,10 +23,10 @@
     )
 
 
-def product(rows, held, plane, which, columns=slice(None)):
+def product(rows, held, plane, which):
     n_task = lax.axis_size("task")
     left = rows[pl.ds(plane * n_task, n_task), which]
-    right = held[which, pl.ds(plane * 2 * n_task, 2 * n_task), :, columns]
+    right = held[which, pl.ds(plane * 2 * n_task, 2 * n_task)]
     depth = left.shape[0] * left.shape[1]
     return lax.dot_general(
         left.reshape(depth, left.shape[2]), right.reshape(depth, right.shape[2]),
@@ -34,20 +34,31 @@
     )
 
 
+def band_edges(width):
+    unit = 2 * LANES
+    half = width // 2 // unit * unit
+    return (0, unit, half, width), (0, width - half, width - unit, width)
+
+
 def last_kernel(held, rows, total, out_attn, out_mlp, staged, sent):
     row_count, column_band = out_attn.shape[1], out_attn.shape[2]
     plane = planes_in_product_order()[3]
     factor = 1.0 / (lax.axis_size("tok") * held.shape[2])
-    n_bands = sent.shape[1]
-    width = column_band // n_bands
+    n_task = lax.axis_size("task")
+    edges = band_edges(column_band)
     writes = []
     for which, out in ((0, out_attn), (1, out_mlp)):
-        for band in range(n_bands):
-            span = slice(band * width, (band + 1) * width)
-            piece = total[which, :, span] + product(rows, held, plane, which, span)
+        left = rows[pl.ds(plane * n_task, n_task), which]
+        left = left.reshape(-1, left.shape[2]).T
+        for low, high in zip(edges[which], edges[which][1:]):
+            span = slice(low, high)
+            right = held[which, pl.ds(plane * 2 * n_task, 2 * n_task), :, span]
+            piece = total[which, :, span] + jnp.dot(
+                left, right.reshape(-1, high - low), preferred_element_type=jnp.float32
+            )
             staged[which, 0, :, span] = piece[:row_count] * factor
             write = pltpu.make_async_copy(
-                staged.at[which, :, :, span], out.at[:, :, span], sent.at[which, band]
+                staged.at[which, :, :, span], out.at[:, :, span], sent.at[len(writes)]
             )
             write.start()
             writes.append(write)
@@ -58,7 +69,8 @@
 def gather_kernel(
     hidden_hbm, attn_hbm, gain_attn_hbm, gain_mlp_hbm, lengths_hbm, held, rows, total,
     hidden, attn_out, gain_attn, gain_mlp, lengths, mine, lent, passing, rising,
-    loaded, ready, z_got, pass_got, rise_got, first_got, second_got, diagonal_got, pair_got, row_got, sent, row_sent,
+    loaded, ready, z_got, pass_got, rise_got, first_got, second_got, diagonal_got, late_got, pair_got,
+    row_got, sent, row_sent,
 ):
     task, tok = lax.axis_index("task"), lax.axis_index("tok")
     n_task = lax.axis_size("task")
@@ -114,6 +126,12 @@
 
     for peer in (to_x, to_y, to_pair):
         signal(barrier, peer)
+
+    @pl.when(core == 1)
+    def _():
+        for tasks in (task_x, task_y):
+            signal(barrier, at(tasks, plane, 0))
+
     for peer, planes, met, _ in z_peers:
         @pl.when(jnp.logical_and(met, planes > plane))
         def _(peer=peer):
@@ -121,12 +139,6 @@
 
     for load in loads:
         load.wait()
-    pl.semaphore_wait(barrier, 3 + jnp.minimum(plane, 2))
-    for reach, (peer, planes, _, answer) in enumerate(z_peers):
-        @pl.when(jnp.logical_and(answer, planes < plane))
-        def _(reach=reach, peer=peer):
-            signal(ready.at[reach], peer)
-
     slab = 16
     seq_count = lengths.shape[1]
     seq_slots = tok_dev * lax.axis_size("tok") // seq_count
@@ -146,6 +158,11 @@
                 mine[which, side, part, :] = done[:, side * column_band : (side + 1) * column_band]
     for which in range(2):
         held[which, own] = mine[which, band]
+    pl.semaphore_wait(barrier, 5 - 2 * core + jnp.minimum(plane, 2))
+    for reach, (peer, planes, _, answer) in enumerate(z_peers):
+        @pl.when(jnp.logical_and(answer, planes < plane))
+        def _(reach=reach, peer=peer):
+            signal(ready.at[reach], peer)
 
     def copy(source, which, q, got, peer):
         return pltpu.make_async_remote_copy(
@@ -259,11 +276,35 @@
                     passing.at[which], held.at[which, q], sent.at[1], z_got.at[which, 2], to_3
                 ).start()
 
+    early_rows, late_rows = pl.ds(0, tok_dev // 2), pl.ds(tok_dev // 2, tok_dev // 2)
+
+    def part_copy(which, q, part, got, peer):
+        span = held.at[which, q, part]
+        pltpu.make_async_remote_copy(
+            src_ref=span, dst_ref=span, send_sem=sent.at[0], recv_sem=got, device_id=peer,
+            device_id_type=pl.DeviceIdType.MESH,
+        ).start()
+
     def first_side(step):
-        for which, tasks, member, axis, peer in ((0, task_x, 1, 0, to_y), (1, task_y, 2, 1, to_x)):
+        def relay_whole(which, q, peer):
+            send(held.at[which, q], which, q, diagonal_got.at[step], peer)
+
+        for which, tasks, member, axis, towards in ((0, task_x, 1, 0, task_y), (1, task_y, 2, 1, task_x)):
             q = chunk(order[step], tasks, core)
+            peer = at(towards, plane, core)
             arrived(held.at[which, q], first_got.at[axis, step])
-            send(held.at[which, q], which, q, diagonal_got.at[step], peer)
+            if step < n_planes - 1:
+                relay_whole(which, q, peer)
+            else:
+                @pl.when(core == 1)
+                def _(which=which, q=q, peer=peer):
+                    relay_whole(which, q, peer)
+
+                @pl.when(core == 0)
+                def _(which=which, q=q, peer=peer, towards=towards):
+                    part_copy(which, q, early_rows, diagonal_got.at[step], peer)
+                    part_copy(which, q, late_rows, late_got.at[0], peer)
+                    part_copy(which, q, late_rows, late_got.at[0], at(towards, plane, 1))
             pair_copy(step, member, which, q, held.at[which, q])
 
     def second_side(step):
@@ -280,9 +321,18 @@
             pair_copy(step, 3, which, q, held.at[which, q])
 
     def diagonal_last(now):
-        @pl.when(now)
-        def _():
-            diagonal_step(n_planes - 1)
+        last = n_planes - 1
+
+        @pl.when(jnp.logical_and(now, core == 1))
+        def _():
+            diagonal_step(last)
+
+        @pl.when(jnp.logical_and(now, core == 0))
+        def _():
+            q = chunk(order[last], task_d, 0)
+            arrived(held.at[:, pl.ds(q, 1), early_rows], diagonal_got.at[last])
+            for which in range(2):
+                part_copy(which, q, early_rows, pair_got.at[last + 1], to_pair)
 
     row_count = column_band // 2 // n_task
     padded = rows.shape[3]
@@ -308,7 +358,20 @@
     def cut(step, members):
         low = chunk(order[step], 0, 0)
         span = held.at[:, pl.ds(low, len(members))]
-        arrived(span, pair_got.at[step if step < n_planes - 1 else n_planes - 1 + members[0] // 3])
+        if (step, members) != (n_planes - 1, (3,)):
+            arrived(span, pair_got.at[min(step, n_planes - 1)])
+        else:
+            half = held.at[:, pl.ds(low, 1), late_rows]
+            arrived(half, late_got.at[0])
+
+            @pl.when(core == 0)
+            def _():
+                arrived(span, pair_got.at[n_planes])
+
+            @pl.when(core == 1)
+            def _():
+                arrived(half, pair_got.at[n_planes])
+
         for member in members:
             tasks = everyone[member]
             group = order[step] * n_task + tasks
@@ -368,6 +431,12 @@
                 total[which] = piece
             else:
                 total[which] += piece
+
+    def cut_and_give(step, cores):
+        @pl.when(core == cores)
+        def _():
+            cut(step, every)
+            give_rows(step, every)
 
     every = (0, 1, 2, 3)
     own_step(0)
@@ -396,9 +465,9 @@
     multiply(0)
     diagonal_step(2)
     lend_rows(1, every)
+    cut_and_give(2, 0)
     first_side(3)
-    cut(2, every)
-    give_rows(2, every)
+    cut_and_give(2, 1)
     multiply(1)
     second_side(3)
     diagonal_last(inner)
@@ -468,6 +537,7 @@
             semaphores((2, 4)),
             semaphores((4,)),
             semaphores((4,)),
+            semaphores((1,)),
             semaphores((5,)),
             semaphores((4,)),
             semaphores((3,)),
@@ -481,7 +551,6 @@
         for array in (hidden, attn_out, gain_attn, gain_mlp, lengths)
     ))
     shape = (1, row_count, column_band)
-    n_bands = column_band // (2 * LANES)
     return pl.pallas_call(
         last_kernel,
         out_shape=(jax.ShapeDtypeStruct(shape, jnp.float32),) * 2,
@@ -489,7 +558,7 @@
         out_specs=(hbm, hbm),
         scratch_shapes=[
             pltpu.VMEM((2,) + shape, jnp.float32),
-            semaphores((2, n_bands)),
+            semaphores((6,)),
         ],
         compiler_params=pltpu.CompilerParams(vmem_limit_bytes=12 * 2**20),
     )(held, rows, total)
@@ -517,7 +586,7 @@
     n_task = lax.axis_size("task")
     block_side = min(4, max(2, n_tok // 16))
     token_parts = n_tok // (block_side * block_side)
-    if (n_task, n_tok, block_side) == (4, 8, 2) and width % (4 * LANES) == 0 and tok_dev % 16 == 0:
+    if (n_task, n_tok, block_side) == (4, 8, 2) and width % (4 * LANES) == 0 and tok_dev % 32 == 0:
         return gathered(hidden, attn_out, gain_attn, gain_mlp, lengths)
     column_band = width // block_side
     tile_rows = column_band // token_parts

time: 39.4 us -> 38.5 us (0.977)
  Pallas kernels: 38.6 us -> 37.7 us
    pallas_call x1, Pallas kernels: 36.5 us -> 35.7 us  [gathered(): pl.pallas_call(gather_kernel, out_shape=(jax.ShapeDtypeStruct((2, devices...]
where the time goes in v3:
time: 38.5 us; the launch traced here: 38.3 us
  Pallas kernels  37.7 us (98%)
  between operations  0.64 us (2%)
    pallas_call x1, Pallas kernels, gathered(): pl.pallas_call(gather_kernel, out_shape=(jax.ShapeDtypeStruct((2, devices...  35.7 us
    pallas_call x1, Pallas kernels, gathered(): pl.pallas_call(last_kernel, out_shape=(jax.ShapeDtypeStruct(shape, jnp.fl...  2 us

profile of v3, /device:TPU:0, one launch (start us, length us, event | category | flops | bytes accessed | tf_op | source)
XLA Modules:
  0.0 38.3 jit_solution(17296628533168077464)
XLA Ops:
  0.6 35.7 %shard_map.68 = (bf16[2,32,32,1792]{3,2,1,0:T(8,128)(2,1)S(1)}, bf16[16,2,64,256]{3,2,1,0:T(8,128)(2,1)S(1)}, f32[2,256,1792]{2,1,0:T(8,128)S(1)}) custom-call(bf16[1,32,3584]{2,1,0:T(8,128)(2,1)} %hidden_hbm.1, bf16[1,32,3584]{2,1,0:T(8,128)(2,1)} %attn_hbm.1, bf16[3584]{0:T(1024)(128)(2,1)} %gain_attn_hbm.1, bf16[3584]{0:T(1024)(128)(2,1)} %gain_mlp_hbm.1, ...), custom_call_target="tpu_custom_call" | custom-call | tf_op jit(solution)/shard_map/pallas_call | solution.py:513
  36.3 2.0 %shard_map.69 = (f32[1,224,1792]{2,1,0:T(8,128)}, f32[1,224,1792]{2,1,0:T(8,128)}) custom-call(bf16[2,32,32,1792]{3,2,1,0:T(8,128)(2,1)S(1)} %get-tuple-element.5.held, bf16[16,2,64,256]{3,2,1,0:T(8,128)(2,1)S(1)} %get-tuple-element.6.rows, f32[2,256,1792]{2,1,0:T(8,128)S(1)} %get-tuple-element.7.total), custom_call_target="tpu_custom_call" | custom-call | tf_op jit(solution)/shard_map/pallas_call | solution.py:554

commit v4 on v3

--- a/solution.py
+++ b/solution.py
@@ -46,7 +46,6 @@
     factor = 1.0 / (lax.axis_size("tok") * held.shape[2])
     n_task = lax.axis_size("task")
     edges = band_edges(column_band)
-    writes = []
     for which, out in ((0, out_attn), (1, out_mlp)):
         left = rows[pl.ds(plane * n_task, n_task), which]
         left = left.reshape(-1, left.shape[2]).T
@@ -57,19 +56,17 @@
                 left, right.reshape(-1, high - low), preferred_element_type=jnp.float32
             )
             staged[which, 0, :, span] = piece[:row_count] * factor
-            write = pltpu.make_async_copy(
-                staged.at[which, :, :, span], out.at[:, :, span], sent.at[len(writes)]
-            )
-            write.start()
-            writes.append(write)
-    for write in writes:
-        write.wait()
+            pltpu.make_async_copy(
+                staged.at[which, :, :, span], out.at[:, :, span], sent.at[which]
+            ).start()
+    for which, out in ((0, out_attn), (1, out_mlp)):
+        pltpu.make_async_copy(staged.at[which], out, sent.at[which]).wait()
 
 
 def gather_kernel(
     hidden_hbm, attn_hbm, gain_attn_hbm, gain_mlp_hbm, lengths_hbm, held, rows, total,
-    hidden, attn_out, gain_attn, gain_mlp, lengths, mine, lent, passing, rising,
-    loaded, ready, z_got, pass_got, rise_got, first_got, second_got, diagonal_got, late_got, pair_got,
+    inputs, gain_attn, gain_mlp, lengths, mine, lent, passing, rising,
+    loaded, ready, z_got, pass_got, rise_got, first_got, second_got, diagonal_got, early_got, late_got, pair_got,
     row_got, sent, row_sent,
 ):
     task, tok = lax.axis_index("task"), lax.axis_index("tok")
@@ -102,16 +99,6 @@
     to_x, to_y, to_pair = at(task_x, plane, core), at(task_y, plane, core), at(task, plane, 1 - core)
     to_1, to_2, to_3 = at(task, plane_1, core), at(task, plane_2, core), at(task, plane_3, core)
 
-    loads = [
-        pltpu.make_async_copy(source, target, loaded.at[spot])
-        for spot, (source, target) in enumerate((
-            (hidden_hbm, hidden), (attn_hbm, attn_out), (gain_attn_hbm, gain_attn),
-            (gain_mlp_hbm, gain_mlp), (lengths_hbm, lengths),
-        ))
-    ]
-    for load in loads:
-        load.start()
-
     barrier = pltpu.get_barrier_semaphore()
     always, odd = plane >= 0, plane % 2 == 1
     z_peers = (
@@ -124,6 +111,12 @@
             semaphore, inc=1, device_id=peer, device_id_type=pl.DeviceIdType.MESH
         )
 
+    for spot, source, target in (
+        (0, hidden_hbm, inputs.at[pl.ds(0, 1)]), (0, attn_hbm, inputs.at[pl.ds(1, 1)]),
+        (1, gain_attn_hbm, gain_attn), (2, gain_mlp_hbm, gain_mlp),
+        (3, lengths_hbm, lengths),
+    ):
+        pltpu.make_async_copy(source, target, loaded.at[spot]).start()
     for peer in (to_x, to_y, to_pair):
         signal(barrier, peer)
 
@@ -137,8 +130,10 @@
         def _(peer=peer):
             signal(barrier, peer)
 
-    for load in loads:
-        load.wait()
+    pltpu.make_async_copy(inputs, inputs, loaded.at[0]).wait()
+    pltpu.make_async_copy(gain_attn_hbm, gain_attn, loaded.at[1]).wait()
+    pltpu.make_async_copy(gain_mlp_hbm, gain_mlp, loaded.at[2]).wait()
+    pltpu.make_async_copy(lengths_hbm, lengths, loaded.at[3]).wait()
     slab = 16
     seq_count = lengths.shape[1]
     seq_slots = tok_dev * lax.axis_size("tok") // seq_count
@@ -150,8 +145,8 @@
             offset = place - seq * seq_slots
             inside = (offset >= 0) & (offset < seq_slots) & (offset < lengths[0, seq])
             live = jnp.where(inside, 1.0, live)
-        first = hidden[0, part, :].astype(jnp.float32)
-        mixed = first + attn_out[0, part, :].astype(jnp.float32)
+        first = inputs[0, part, :].astype(jnp.float32)
+        mixed = first + inputs[1, part, :].astype(jnp.float32)
         for which, values, gain in ((0, first, gain_attn), (1, mixed, gain_mlp)):
             done = (normed(values, gain[...].reshape(1, -1)) * live).astype(jnp.bfloat16)
             for side in range(2):
@@ -162,7 +157,7 @@
     for reach, (peer, planes, _, answer) in enumerate(z_peers):
         @pl.when(jnp.logical_and(answer, planes < plane))
         def _(reach=reach, peer=peer):
-            signal(ready.at[reach], peer)
+            signal(ready.at[reach % 2], peer)
 
     def copy(source, which, q, got, peer):
         return pltpu.make_async_remote_copy(
@@ -190,8 +185,10 @@
             return held.at[which, q] if step else mine.at[which, band]
 
         def landed(which):
-            if step:
-                arrived(held.at[which, q], z_got.at[which, step - 1])
+            if step == 1:
+                arrived(held.at[which, q], z_got.at[which])
+            elif step and which == 0:
+                arrived(held.at[:, pl.ds(q, 1)], z_got.at[step])
 
         landed(0)
         send(source(0), 0, q, first_got.at[0, step], to_x)
@@ -207,25 +204,25 @@
 
         @pl.when(jnp.logical_and(answer, planes > plane))
         def _():
-            pl.semaphore_wait(ready.at[reach], 1)
+            pl.semaphore_wait(ready.at[reach % 2], 1)
 
     def inward(planes):
         @pl.when(plane == planes)
         def _():
             for which in range(2):
-                send(mine.at[which, 1 - band], which, own, z_got.at[which, 1], to_3)
+                send(mine.at[which, 1 - band], which, own, z_got.at[2], to_3)
 
     def z_sends():
         inward(2)
         answered(0)
         for which in range(2):
-            send(mine.at[which, 1 - band], which, own, z_got.at[which, 0], to_1)
+            send(mine.at[which, 1 - band], which, own, z_got.at[which], to_1)
 
         @pl.when(outer)
         def _():
             for which in range(2):
                 outward(
-                    mine.at[which, band], passing.at[which], sent.at[0], pass_got.at[which], to_1
+                    mine.at[which, band], passing.at[which], sent.at[0], pass_got.at[0], to_1
                 ).start()
 
         answered(2)
@@ -234,13 +231,13 @@
         def _():
             for which in range(2):
                 outward(
-                    mine.at[which, band], rising.at[which], sent.at[0], rise_got.at[which], to_3
+                    mine.at[which, band], rising.at[which], sent.at[0], rise_got.at[0], to_3
                 ).start()
 
         @pl.when(plane == 2)
         def _():
             for which in range(2):
-                send(mine.at[which, band], which, own, z_got.at[which, 1], to_2)
+                send(mine.at[which, band], which, own, z_got.at[2], to_2)
 
     def outward(source, target, semaphore, got, peer):
         return pltpu.make_async_remote_copy(
@@ -252,10 +249,10 @@
         @pl.when(plane == 2)
         def _():
             q = chunk(plane_3, task, core)
-            for which in range(2):
-                arrived(rising.at[which], rise_got.at[which])
+            arrived(rising, rise_got.at[0])
+            for which in range(2):
                 outward(
-                    rising.at[which], held.at[which, q], sent.at[2], z_got.at[which, 1], to_1
+                    rising.at[which], held.at[which, q], sent.at[1], z_got.at[2], to_1
                 ).start()
 
     def relay(planes):
@@ -264,24 +261,24 @@
             answered(1)
             q = chunk(plane_1, task, core)
             for which in range(2):
-                send(held.at[which, q], which, q, z_got.at[which, 2], to_2)
+                send(held.at[which, q], which, q, z_got.at[3], to_2)
 
     def pass_on():
         @pl.when(inner)
         def _():
             q = chunk(plane_1, task, core)
-            for which in range(2):
-                arrived(passing.at[which], pass_got.at[which])
+            arrived(passing, pass_got.at[0])
+            for which in range(2):
                 outward(
-                    passing.at[which], held.at[which, q], sent.at[1], z_got.at[which, 2], to_3
+                    passing.at[which], held.at[which, q], sent.at[1], z_got.at[3], to_3
                 ).start()
 
     early_rows, late_rows = pl.ds(0, tok_dev // 2), pl.ds(tok_dev // 2, tok_dev // 2)
 
-    def part_copy(which, q, part, got, peer):
+    def part_copy(which, q, part, spot, got, peer):
         span = held.at[which, q, part]
         pltpu.make_async_remote_copy(
-            src_ref=span, dst_ref=span, send_sem=sent.at[0], recv_sem=got, device_id=peer,
+            src_ref=span, dst_ref=span, send_sem=sent.at[spot], recv_sem=got, device_id=peer,
             device_id_type=pl.DeviceIdType.MESH,
         ).start()
 
@@ -302,9 +299,10 @@
 
                 @pl.when(core == 0)
                 def _(which=which, q=q, peer=peer, towards=towards):
-                    part_copy(which, q, early_rows, diagonal_got.at[step], peer)
-                    part_copy(which, q, late_rows, late_got.at[0], peer)
-                    part_copy(which, q, late_rows, late_got.at[0], at(towards, plane, 1))
+                    twin = at(towards, plane, 1)
+                    part_copy(which, q, early_rows, 0, early_got.at[0], twin)
+                    part_copy(which, q, late_rows, 0, late_got.at[0], peer)
+                    part_copy(which, q, late_rows, 2, late_got.at[0], twin)
             pair_copy(step, member, which, q, held.at[which, q])
 
     def second_side(step):
@@ -320,19 +318,16 @@
         for which in range(2):
             pair_copy(step, 3, which, q, held.at[which, q])
 
-    def diagonal_last(now):
+    def diagonal_last():
         last = n_planes - 1
 
-        @pl.when(jnp.logical_and(now, core == 1))
+        @pl.when(core == 1)
         def _():
             diagonal_step(last)
-
-        @pl.when(jnp.logical_and(now, core == 0))
-        def _():
             q = chunk(order[last], task_d, 0)
-            arrived(held.at[:, pl.ds(q, 1), early_rows], diagonal_got.at[last])
-            for which in range(2):
-                part_copy(which, q, early_rows, pair_got.at[last + 1], to_pair)
+            arrived(held.at[:, pl.ds(q, 1), early_rows], early_got.at[0])
+            for which in range(2):
+                part_copy(which, q, early_rows, 2, pair_got.at[last + 1], to_pair)
 
     row_count = column_band // 2 // n_task
     padded = rows.shape[3]
@@ -366,11 +361,7 @@
 
             @pl.when(core == 0)
             def _():
-                arrived(span, pair_got.at[n_planes])
-
-            @pl.when(core == 1)
-            def _():
-                arrived(half, pair_got.at[n_planes])
+                arrived(held.at[0, pl.ds(0, 3)], pair_got.at[n_planes])
 
         for member in members:
             tasks = everyone[member]
@@ -437,6 +428,16 @@
         def _():
             cut(step, every)
             give_rows(step, every)
+
+    def multiply_when(now, step):
+        @pl.when(now)
+        def _():
+            multiply(step)
+
+    def cut_when(now, step, members):
+        @pl.when(now)
+        def _():
+            cut(step, members)
 
     every = (0, 1, 2, 3)
     own_step(0)
@@ -469,11 +470,12 @@
     first_side(3)
     cut_and_give(2, 1)
     multiply(1)
+    multiply_when(outer, 2)
     second_side(3)
-    diagonal_last(inner)
-    multiply(2)
-    diagonal_last(outer)
-    cut(3, (0, 1, 2))
+    cut_when(jnp.logical_and(outer, core == 0), 3, (0, 1, 2))
+    diagonal_last()
+    multiply_when(inner, 2)
+    cut_when(jnp.logical_or(inner, core == 1), 3, (0, 1, 2))
     cut(3, (3,))
     rows_arrive(3)
 
@@ -483,20 +485,29 @@
             device_id=to_pair, device_id_type=pl.DeviceIdType.MESH,
         ).wait_send()
 
+    chunks = held.shape[1]
+    for cores in range(2):
+        for place, least in ((outer, chunks - 3), (inner, chunks - 1)):
+            @pl.when(jnp.logical_and(place, core == cores))
+            def _(count=least + cores):
+                all_sent(held.at[:, pl.ds(0, count)], sent.at[0])
+
+    all_sent(held.at[0, pl.ds(0, 1)], sent.at[2])
+
+    @pl.when(plane == 1)
+    def _():
+        all_sent(passing, sent.at[1])
+
+    @pl.when(plane == 2)
+    def _():
+        all_sent(mine, sent.at[1])
+
     @pl.when(inner)
     def _():
-        all_sent(held, sent.at[0])
-        all_sent(passing, sent.at[1])
-
-        @pl.when(plane == 2)
-        def _():
-            all_sent(rising, sent.at[2])
-
         all_sent(rows.at[pl.ds(0, len(lends))], row_sent.at[0])
 
     @pl.when(outer)
     def _():
-        all_sent(held.at[:, pl.ds(0, held.shape[1] - 2)], sent.at[0])
         all_sent(rows.at[pl.ds(0, len(gives))], row_sent.at[0])
 
 
@@ -520,8 +531,7 @@
         in_specs=[hbm] * 5,
         out_specs=(vmem,) * 3,
         scratch_shapes=[
-            pltpu.VMEM(hidden.shape, jnp.bfloat16),
-            pltpu.VMEM(attn_out.shape, jnp.bfloat16),
+            pltpu.VMEM((2,) + hidden.shape[1:], jnp.bfloat16),
             pltpu.VMEM(gain_attn.shape, jnp.bfloat16),
             pltpu.VMEM(gain_mlp.shape, jnp.bfloat16),
             pltpu.SMEM(lengths.shape, jnp.int32),
@@ -529,14 +539,15 @@
             pltpu.VMEM((2, n_task, 2, 2 * tok_dev, padded), jnp.bfloat16),
             pltpu.VMEM((2, tok_dev, column_band), jnp.bfloat16),
             pltpu.VMEM((2, tok_dev, column_band), jnp.bfloat16),
-            semaphores((5,)),
-            pltpu.SemaphoreType.REGULAR((3,)),
-            semaphores((2, 3)),
-            semaphores((2,)),
-            semaphores((2,)),
+            semaphores((4,)),
+            pltpu.SemaphoreType.REGULAR((2,)),
+            semaphores((4,)),
+            semaphores((1,)),
+            semaphores((1,)),
             semaphores((2, 4)),
             semaphores((4,)),
             semaphores((4,)),
+            semaphores((1,)),
             semaphores((1,)),
             semaphores((5,)),
             semaphores((4,)),
@@ -558,7 +569,7 @@
         out_specs=(hbm, hbm),
         scratch_shapes=[
             pltpu.VMEM((2,) + shape, jnp.float32),
-            semaphores((6,)),
+            semaphores((2,)),
         ],
         compiler_params=pltpu.CompilerParams(vmem_limit_bytes=12 * 2**20),
     )(held, rows, total)

time: 38.5 us -> 38.4 us (level)
  no operation moved by 1% of the time
where the time goes in v4:
time: 38.4 us; the launch traced here: 38.2 us
  Pallas kernels  37.6 us (98%)
  between operations  0.64 us (2%)
    pallas_call x1, Pallas kernels, gathered(): pl.pallas_call(gather_kernel, out_shape=(jax.ShapeDtypeStruct((2, devices...  35.6 us
    pallas_call x1, Pallas kernels, gathered(): pl.pallas_call(last_kernel, out_shape=(jax.ShapeDtypeStruct(shape, jnp.fl...  1.96 us

profile of v4, /device:TPU:0, one launch (start us, length us, event | category | flops | bytes accessed | tf_op | source)
XLA Modules:
  0.0 38.2 jit_solution(8601471486939067214)
XLA Ops:
  0.6 35.6 %shard_map.68 = (bf16[2,32,32,1792]{3,2,1,0:T(8,128)(2,1)S(1)}, bf16[16,2,64,256]{3,2,1,0:T(8,128)(2,1)S(1)}, f32[2,256,1792]{2,1,0:T(8,128)S(1)}) custom-call(bf16[1,32,3584]{2,1,0:T(8,128)(2,1)} %hidden_hbm.1, bf16[1,32,3584]{2,1,0:T(8,128)(2,1)} %attn_hbm.1, bf16[3584]{0:T(1024)(128)(2,1)} %gain_attn_hbm.1, bf16[3584]{0:T(1024)(128)(2,1)} %gain_mlp_hbm.1, ...), custom_call_target="tpu_custom_call" | custom-call | tf_op jit(solution)/shard_map/pallas_call | solution.py:524
  36.2 2.0 %shard_map.69 = (f32[1,224,1792]{2,1,0:T(8,128)}, f32[1,224,1792]{2,1,0:T(8,128)}) custom-call(bf16[2,32,32,1792]{3,2,1,0:T(8,128)(2,1)S(1)} %get-tuple-element.5.held, bf16[16,2,64,256]{3,2,1,0:T(8,128)(2,1)S(1)} %get-tuple-element.6.rows, f32[2,256,1792]{2,1,0:T(8,128)S(1)} %get-tuple-element.7.total), custom_call_target="tpu_custom_call" | custom-call | tf_op jit(solution)/shard_map/pallas_call | solution.py:565

commit v5 on v4

--- a/solution.py
+++ b/solution.py
@@ -45,20 +45,35 @@
     plane = planes_in_product_order()[3]
     factor = 1.0 / (lax.axis_size("tok") * held.shape[2])
     n_task = lax.axis_size("task")
-    edges = band_edges(column_band)
-    for which, out in ((0, out_attn), (1, out_mlp)):
+    outs = (out_attn, out_mlp)
+    lefts = []
+    for which in range(2):
         left = rows[pl.ds(plane * n_task, n_task), which]
-        left = left.reshape(-1, left.shape[2]).T
-        for low, high in zip(edges[which], edges[which][1:]):
-            span = slice(low, high)
-            right = held[which, pl.ds(plane * 2 * n_task, 2 * n_task), :, span]
-            piece = total[which, :, span] + jnp.dot(
-                left, right.reshape(-1, high - low), preferred_element_type=jnp.float32
-            )
-            staged[which, 0, :, span] = piece[:row_count] * factor
-            pltpu.make_async_copy(
-                staged.at[which, :, :, span], out.at[:, :, span], sent.at[which]
-            ).start()
+        lefts.append(left.reshape(-1, left.shape[2]).T[:row_count])
+    bands = [
+        (which, low, high)
+        for which, edges in enumerate(band_edges(column_band))
+        for low, high in zip(edges, edges[1:])
+    ]
+
+    def multiplied(which, low, high):
+        right = held[which, pl.ds(plane * 2 * n_task, 2 * n_task), :, low:high]
+        return jnp.dot(
+            lefts[which], right.reshape(-1, high - low), preferred_element_type=jnp.float32
+        )
+
+    def put(piece, which, low, high):
+        span = slice(low, high)
+        staged[which, 0, :, span] = (total[which, :row_count, span] + piece) * factor
+        pltpu.make_async_copy(
+            staged.at[which, :, :, span], outs[which].at[:, :, span], sent.at[which]
+        ).start()
+
+    ahead = multiplied(*bands[0])
+    for band, later in zip(bands, bands[1:]):
+        piece, ahead = ahead, multiplied(*later)
+        put(piece, *band)
+    put(ahead, *bands[-1])
     for which, out in ((0, out_attn), (1, out_mlp)):
         pltpu.make_async_copy(staged.at[which], out, sent.at[which]).wait()
 
@@ -134,7 +149,7 @@
     pltpu.make_async_copy(gain_attn_hbm, gain_attn, loaded.at[1]).wait()
     pltpu.make_async_copy(gain_mlp_hbm, gain_mlp, loaded.at[2]).wait()
     pltpu.make_async_copy(lengths_hbm, lengths, loaded.at[3]).wait()
-    slab = 16
+    slab = 8
     seq_count = lengths.shape[1]
     seq_slots = tok_dev * lax.axis_size("tok") // seq_count
     for low in range(0, tok_dev, slab):
@@ -148,7 +163,9 @@
         first = inputs[0, part, :].astype(jnp.float32)
         mixed = first + inputs[1, part, :].astype(jnp.float32)
         for which, values, gain in ((0, first, gain_attn), (1, mixed, gain_mlp)):
-            done = (normed(values, gain[...].reshape(1, -1)) * live).astype(jnp.bfloat16)
+            scale = lax.rsqrt(jnp.mean(values * values, axis=-1, keepdims=True) + 1e-06) * live
+            weight = gain[...].reshape(1, -1).astype(jnp.float32)
+            done = (values * scale * weight).astype(jnp.bfloat16)
             for side in range(2):
                 mine[which, side, part, :] = done[:, side * column_band : (side + 1) * column_band]
     for which in range(2):

time: 38.4 us -> 38.3 us (level)
  no operation moved by 1% of the time
where the time goes in v5:
time: 38.3 us; the launch traced here: 38.2 us
  Pallas kernels  37.5 us (98%)
  between operations  0.64 us (2%)
    pallas_call x1, Pallas kernels, gathered(): pl.pallas_call(gather_kernel, out_shape=(jax.ShapeDtypeStruct((2, devices...  35.6 us
    pallas_call x1, Pallas kernels, gathered(): pl.pallas_call(last_kernel, out_shape=(jax.ShapeDtypeStruct(shape, jnp.fl...  1.97 us

profile of v5, /device:TPU:0, one launch (start us, length us, event | category | flops | bytes accessed | tf_op | source)
XLA Modules:
  0.0 38.2 jit_solution(5107846638301745023)
XLA Ops:
  0.6 35.6 %shard_map.68 = (bf16[2,32,32,1792]{3,2,1,0:T(8,128)(2,1)S(1)}, bf16[16,2,64,256]{3,2,1,0:T(8,128)(2,1)S(1)}, f32[2,256,1792]{2,1,0:T(8,128)S(1)}) custom-call(bf16[1,32,3584]{2,1,0:T(8,128)(2,1)} %hidden_hbm.1, bf16[1,32,3584]{2,1,0:T(8,128)(2,1)} %attn_hbm.1, bf16[3584]{0:T(1024)(128)(2,1)} %gain_attn_hbm.1, bf16[3584]{0:T(1024)(128)(2,1)} %gain_mlp_hbm.1, ...), custom_call_target="tpu_custom_call" | custom-call | tf_op jit(solution)/shard_map/pallas_call | solution.py:541
  36.2 2.0 %shard_map.69 = (f32[1,224,1792]{2,1,0:T(8,128)}, f32[1,224,1792]{2,1,0:T(8,128)}) custom-call(bf16[2,32,32,1792]{3,2,1,0:T(8,128)(2,1)S(1)} %get-tuple-element.5.held, bf16[16,2,64,256]{3,2,1,0:T(8,128)(2,1)S(1)} %get-tuple-element.6.rows, f32[2,256,1792]{2,1,0:T(8,128)S(1)} %get-tuple-element.7.total), custom_call_target="tpu_custom_call" | custom-call | tf_op jit(solution)/shard_map/pallas_call | solution.py:582

commit v6 on v5

--- a/solution.py
+++ b/solution.py
@@ -152,29 +152,48 @@
     slab = 8
     seq_count = lengths.shape[1]
     seq_slots = tok_dev * lax.axis_size("tok") // seq_count
-    for low in range(0, tok_dev, slab):
-        part = pl.ds(low, slab)
-        place = tok * tok_dev + low + lax.broadcasted_iota(jnp.int32, (slab, 1), 0)
-        live = jnp.zeros((slab, 1), jnp.float32)
-        for seq in range(seq_count):
-            offset = place - seq * seq_slots
-            inside = (offset >= 0) & (offset < seq_slots) & (offset < lengths[0, seq])
-            live = jnp.where(inside, 1.0, live)
-        first = inputs[0, part, :].astype(jnp.float32)
-        mixed = first + inputs[1, part, :].astype(jnp.float32)
-        for which, values, gain in ((0, first, gain_attn), (1, mixed, gain_mlp)):
-            scale = lax.rsqrt(jnp.mean(values * values, axis=-1, keepdims=True) + 1e-06) * live
-            weight = gain[...].reshape(1, -1).astype(jnp.float32)
-            done = (values * scale * weight).astype(jnp.bfloat16)
-            for side in range(2):
-                mine[which, side, part, :] = done[:, side * column_band : (side + 1) * column_band]
-    for which in range(2):
-        held[which, own] = mine[which, band]
+    half = tok_dev // 2
+    early_rows, late_rows = pl.ds(0, half), pl.ds(half, half)
+
+    def norm_rows(start, part):
+        for low in range(start, start + half, slab):
+            spot = pl.ds(low, slab)
+            place = tok * tok_dev + low + lax.broadcasted_iota(jnp.int32, (slab, 1), 0)
+            live = jnp.zeros((slab, 1), jnp.float32)
+            for seq in range(seq_count):
+                offset = place - seq * seq_slots
+                inside = (offset >= 0) & (offset < seq_slots) & (offset < lengths[0, seq])
+                live = jnp.where(inside, 1.0, live)
+            first = inputs[0, spot, :].astype(jnp.float32)
+            mixed = first + inputs[1, spot, :].astype(jnp.float32)
+            for which, values, gain in ((0, first, gain_attn), (1, mixed, gain_mlp)):
+                mean = jnp.mean(values * values, axis=-1, keepdims=True)
+                scale = lax.rsqrt(mean + 1e-06) * live
+                weight = gain[...].reshape(1, -1).astype(jnp.float32)
+                done = (values * scale * weight).astype(jnp.bfloat16)
+                for side in range(2):
+                    span = slice(side * column_band, (side + 1) * column_band)
+                    mine[which, side, spot, :] = done[:, span]
+        for which in range(2):
+            held[which, own, part] = mine[which, band, part]
+
+    def first_copies(part):
+        for which, peer in ((0, to_x), (1, to_y)):
+            pltpu.make_async_remote_copy(
+                src_ref=mine.at[which, band, part], dst_ref=held.at[which, own, part],
+                send_sem=sent.at[0], recv_sem=first_got.at[which, 0], device_id=peer,
+                device_id_type=pl.DeviceIdType.MESH,
+            ).start()
+
+    norm_rows(0, early_rows)
     pl.semaphore_wait(barrier, 5 - 2 * core + jnp.minimum(plane, 2))
+    first_copies(early_rows)
     for reach, (peer, planes, _, answer) in enumerate(z_peers):
         @pl.when(jnp.logical_and(answer, planes < plane))
         def _(reach=reach, peer=peer):
             signal(ready.at[reach % 2], peer)
+    norm_rows(half, late_rows)
+    first_copies(late_rows)
 
     def copy(source, which, q, got, peer):
         return pltpu.make_async_remote_copy(
@@ -208,10 +227,12 @@
                 arrived(held.at[:, pl.ds(q, 1)], z_got.at[step])
 
         landed(0)
-        send(source(0), 0, q, first_got.at[0, step], to_x)
+        if step:
+            send(source(0), 0, q, first_got.at[0, step], to_x)
         pair_copy(step, 0, 0, q, source(0))
         landed(1)
-        send(source(1), 1, q, first_got.at[1, step], to_y)
+        if step:
+            send(source(1), 1, q, first_got.at[1, step], to_y)
         send(source(1), 1, q, second_got.at[step], to_x)
         send(source(0), 0, q, second_got.at[step], to_y)
         pair_copy(step, 0, 1, q, source(1))
@@ -289,8 +310,6 @@
                 outward(
                     passing.at[which], held.at[which, q], sent.at[1], z_got.at[3], to_3
                 ).start()
-
-    early_rows, late_rows = pl.ds(0, tok_dev // 2), pl.ds(tok_dev // 2, tok_dev // 2)
 
     def part_copy(which, q, part, spot, got, peer):
         span = held.at[which, q, part]

time: 38.3 us -> 38.3 us (level)
  no operation moved by 1% of the time
where the time goes in v6:
time: 38.3 us; the launch traced here: 38.1 us
  Pallas kernels  37.5 us (98%)
  between operations  0.64 us (2%)
    pallas_call x1, Pallas kernels, gathered(): pl.pallas_call(gather_kernel, out_shape=(jax.ShapeDtypeStruct((2, devices...  35.5 us
    pallas_call x1, Pallas kernels, gathered(): pl.pallas_call(last_kernel, out_shape=(jax.ShapeDtypeStruct(shape, jnp.fl...  1.97 us

profile of v6, /device:TPU:0, one launch (start us, length us, event | category | flops | bytes accessed | tf_op | source)
XLA Modules:
  0.0 38.1 jit_solution(11277660204906212364)
XLA Ops:
  0.6 35.5 %shard_map.68 = (bf16[2,32,32,1792]{3,2,1,0:T(8,128)(2,1)S(1)}, bf16[16,2,64,256]{3,2,1,0:T(8,128)(2,1)S(1)}, f32[2,256,1792]{2,1,0:T(8,128)S(1)}) custom-call(bf16[1,32,3584]{2,1,0:T(8,128)(2,1)} %hidden_hbm.1, bf16[1,32,3584]{2,1,0:T(8,128)(2,1)} %attn_hbm.1, bf16[3584]{0:T(1024)(128)(2,1)} %gain_attn_hbm.1, bf16[3584]{0:T(1024)(128)(2,1)} %gain_mlp_hbm.1, ...), custom_call_target="tpu_custom_call" | custom-call | tf_op jit(solution)/shard_map/pallas_call | solution.py:560
  36.1 2.0 %shard_map.69 = (f32[1,224,1792]{2,1,0:T(8,128)}, f32[1,224,1792]{2,1,0:T(8,128)}) custom-call(bf16[2,32,32,1792]{3,2,1,0:T(8,128)(2,1)S(1)} %get-tuple-element.5.held, bf16[16,2,64,256]{3,2,1,0:T(8,128)(2,1)S(1)} %get-tuple-element.6.rows, f32[2,256,1792]{2,1,0:T(8,128)S(1)} %get-tuple-element.7.total), custom_call_target="tpu_custom_call" | custom-call | tf_op jit(solution)/shard_map/pallas_call | solution.py:601

commit v7 on v5

--- a/solution.py
+++ b/solution.py
@@ -81,7 +81,7 @@
 def gather_kernel(
     hidden_hbm, attn_hbm, gain_attn_hbm, gain_mlp_hbm, lengths_hbm, held, rows, total,
     inputs, gain_attn, gain_mlp, lengths, mine, lent, passing, rising,
-    loaded, ready, z_got, pass_got, rise_got, first_got, second_got, diagonal_got, early_got, late_got, pair_got,
+    ready, z_got, pass_got, rise_got, first_got, second_got, diagonal_got, early_got, late_got, pair_got,
     row_got, sent, row_sent,
 ):
     task, tok = lax.axis_index("task"), lax.axis_index("tok")
@@ -126,12 +126,13 @@
             semaphore, inc=1, device_id=peer, device_id_type=pl.DeviceIdType.MESH
         )
 
-    for spot, source, target in (
-        (0, hidden_hbm, inputs.at[pl.ds(0, 1)]), (0, attn_hbm, inputs.at[pl.ds(1, 1)]),
-        (1, gain_attn_hbm, gain_attn), (2, gain_mlp_hbm, gain_mlp),
-        (3, lengths_hbm, lengths),
+    for semaphore, source, target in (
+        (sent.at[0], hidden_hbm, inputs.at[pl.ds(0, 1)]),
+        (sent.at[0], attn_hbm, inputs.at[pl.ds(1, 1)]),
+        (sent.at[1], gain_attn_hbm, gain_attn), (sent.at[2], gain_mlp_hbm, gain_mlp),
+        (row_sent.at[0], lengths_hbm, lengths),
     ):
-        pltpu.make_async_copy(source, target, loaded.at[spot]).start()
+        pltpu.make_async_copy(source, target, semaphore).start()
     for peer in (to_x, to_y, to_pair):
         signal(barrier, peer)
 
@@ -145,10 +146,10 @@
         def _(peer=peer):
             signal(barrier, peer)
 
-    pltpu.make_async_copy(inputs, inputs, loaded.at[0]).wait()
-    pltpu.make_async_copy(gain_attn_hbm, gain_attn, loaded.at[1]).wait()
-    pltpu.make_async_copy(gain_mlp_hbm, gain_mlp, loaded.at[2]).wait()
-    pltpu.make_async_copy(lengths_hbm, lengths, loaded.at[3]).wait()
+    pltpu.make_async_copy(inputs, inputs, sent.at[0]).wait()
+    pltpu.make_async_copy(gain_attn_hbm, gain_attn, sent.at[1]).wait()
+    pltpu.make_async_copy(gain_mlp_hbm, gain_mlp, sent.at[2]).wait()
+    pltpu.make_async_copy(lengths_hbm, lengths, row_sent.at[0]).wait()
     slab = 8
     seq_count = lengths.shape[1]
     seq_slots = tok_dev * lax.axis_size("tok") // seq_count
@@ -556,7 +557,6 @@
             pltpu.VMEM((2, n_task, 2, 2 * tok_dev, padded), jnp.bfloat16),
             pltpu.VMEM((2, tok_dev, column_band), jnp.bfloat16),
             pltpu.VMEM((2, tok_dev, column_band), jnp.bfloat16),
-            semaphores((4,)),
             pltpu.SemaphoreType.REGULAR((2,)),
             semaphores((4,)),
             semaphores((1,)),

time: 38.3 us -> 38.3 us (level)
  no operation moved by 1% of the time
where the time goes in v7:
time: 38.3 us; the launch traced here: 38.1 us
  Pallas kernels  37.5 us (98%)
  between operations  0.64 us (2%)
    pallas_call x1, Pallas kernels, gathered(): pl.pallas_call(gather_kernel, out_shape=(jax.ShapeDtypeStruct((2, devices...  35.5 us
    pallas_call x1, Pallas kernels, gathered(): pl.pallas_call(last_kernel, out_shape=(jax.ShapeDtypeStruct(shape, jnp.fl...  1.96 us

profile of v7, /device:TPU:0, one launch (start us, length us, event | category | flops | bytes accessed | tf_op | source)
XLA Modules:
  0.0 38.1 jit_solution(12242440252147500381)
XLA Ops:
  0.6 35.5 %shard_map.68 = (bf16[2,32,32,1792]{3,2,1,0:T(8,128)(2,1)S(1)}, bf16[16,2,64,256]{3,2,1,0:T(8,128)(2,1)S(1)}, f32[2,256,1792]{2,1,0:T(8,128)S(1)}) custom-call(bf16[1,32,3584]{2,1,0:T(8,128)(2,1)} %hidden_hbm.1, bf16[1,32,3584]{2,1,0:T(8,128)(2,1)} %attn_hbm.1, bf16[3584]{0:T(1024)(128)(2,1)} %gain_attn_hbm.1, bf16[3584]{0:T(1024)(128)(2,1)} %gain_mlp_hbm.1, ...), custom_call_target="tpu_custom_call" | custom-call | tf_op jit(solution)/shard_map/pallas_call | solution.py:542
  36.2 2.0 %shard_map.69 = (f32[1,224,1792]{2,1,0:T(8,128)}, f32[1,224,1792]{2,1,0:T(8,128)}) custom-call(bf16[2,32,32,1792]{3,2,1,0:T(8,128)(2,1)S(1)} %get-tuple-element.5.held, bf16[16,2,64,256]{3,2,1,0:T(8,128)(2,1)S(1)} %get-tuple-element.6.rows, f32[2,256,1792]{2,1,0:T(8,128)S(1)} %get-tuple-element.7.total), custom_call_target="tpu_custom_call" | custom-call | tf_op jit(solution)/shard_map/pallas_call | solution.py:582

commit v8 on v6

--- a/solution.py
+++ b/solution.py
@@ -81,7 +81,7 @@
 def gather_kernel(
     hidden_hbm, attn_hbm, gain_attn_hbm, gain_mlp_hbm, lengths_hbm, held, rows, total,
     inputs, gain_attn, gain_mlp, lengths, mine, lent, passing, rising,
-    loaded, ready, z_got, pass_got, rise_got, first_got, second_got, diagonal_got, early_got, late_got, pair_got,
+    ready, z_got, pass_got, rise_got, first_got, second_got, diagonal_got, early_got, late_got, pair_got,
     row_got, sent, row_sent,
 ):
     task, tok = lax.axis_index("task"), lax.axis_index("tok")
@@ -126,12 +126,13 @@
             semaphore, inc=1, device_id=peer, device_id_type=pl.DeviceIdType.MESH
         )
 
-    for spot, source, target in (
-        (0, hidden_hbm, inputs.at[pl.ds(0, 1)]), (0, attn_hbm, inputs.at[pl.ds(1, 1)]),
-        (1, gain_attn_hbm, gain_attn), (2, gain_mlp_hbm, gain_mlp),
-        (3, lengths_hbm, lengths),
+    for semaphore, source, target in (
+        (sent.at[0], hidden_hbm, inputs.at[pl.ds(0, 1)]),
+        (sent.at[0], attn_hbm, inputs.at[pl.ds(1, 1)]),
+        (sent.at[1], gain_attn_hbm, gain_attn), (sent.at[2], gain_mlp_hbm, gain_mlp),
+        (row_sent.at[0], lengths_hbm, lengths),
     ):
-        pltpu.make_async_copy(source, target, loaded.at[spot]).start()
+        pltpu.make_async_copy(source, target, semaphore).start()
     for peer in (to_x, to_y, to_pair):
         signal(barrier, peer)
 
@@ -145,10 +146,10 @@
         def _(peer=peer):
             signal(barrier, peer)
 
-    pltpu.make_async_copy(inputs, inputs, loaded.at[0]).wait()
-    pltpu.make_async_copy(gain_attn_hbm, gain_attn, loaded.at[1]).wait()
-    pltpu.make_async_copy(gain_mlp_hbm, gain_mlp, loaded.at[2]).wait()
-    pltpu.make_async_copy(lengths_hbm, lengths, loaded.at[3]).wait()
+    pltpu.make_async_copy(inputs, inputs, sent.at[0]).wait()
+    pltpu.make_async_copy(gain_attn_hbm, gain_attn, sent.at[1]).wait()
+    pltpu.make_async_copy(gain_mlp_hbm, gain_mlp, sent.at[2]).wait()
+    pltpu.make_async_copy(lengths_hbm, lengths, row_sent.at[0]).wait()
     slab = 8
     seq_count = lengths.shape[1]
     seq_slots = tok_dev * lax.axis_size("tok") // seq_count
@@ -575,7 +576,6 @@
             pltpu.VMEM((2, n_task, 2, 2 * tok_dev, padded), jnp.bfloat16),
             pltpu.VMEM((2, tok_dev, column_band), jnp.bfloat16),
             pltpu.VMEM((2, tok_dev, column_band), jnp.bfloat16),
-            semaphores((4,)),
             pltpu.SemaphoreType.REGULAR((2,)),
             semaphores((4,)),
             semaphores((1,)),

time: 38.3 us -> 38.2 us (level)
  no operation moved by 1% of the time
where the time goes in v8:
time: 38.2 us; the launch traced here: 38.1 us
  Pallas kernels  37.4 us (98%)
  between operations  0.64 us (2%)
    pallas_call x1, Pallas kernels, gathered(): pl.pallas_call(gather_kernel, out_shape=(jax.ShapeDtypeStruct((2, devices...  35.5 us
    pallas_call x1, Pallas kernels, gathered(): pl.pallas_call(last_kernel, out_shape=(jax.ShapeDtypeStruct(shape, jnp.fl...  1.96 us

profile of v8, /device:TPU:0, one launch (start us, length us, event | category | flops | bytes accessed | tf_op | source)
XLA Modules:
  0.0 38.1 jit_solution(16961885395656224108)
XLA Ops:
  0.6 35.5 %shard_map.68 = (bf16[2,32,32,1792]{3,2,1,0:T(8,128)(2,1)S(1)}, bf16[16,2,64,256]{3,2,1,0:T(8,128)(2,1)S(1)}, f32[2,256,1792]{2,1,0:T(8,128)S(1)}) custom-call(bf16[1,32,3584]{2,1,0:T(8,128)(2,1)} %hidden_hbm.1, bf16[1,32,3584]{2,1,0:T(8,128)(2,1)} %attn_hbm.1, bf16[3584]{0:T(1024)(128)(2,1)} %gain_attn_hbm.1, bf16[3584]{0:T(1024)(128)(2,1)} %gain_mlp_hbm.1, ...), custom_call_target="tpu_custom_call" | custom-call | tf_op jit(solution)/shard_map/pallas_call | solution.py:561
  36.1 2.0 %shard_map.69 = (f32[1,224,1792]{2,1,0:T(8,128)}, f32[1,224,1792]{2,1,0:T(8,128)}) custom-call(bf16[2,32,32,1792]{3,2,1,0:T(8,128)(2,1)S(1)} %get-tuple-element.5.held, bf16[16,2,64,256]{3,2,1,0:T(8,128)(2,1)S(1)} %get-tuple-element.6.rows, f32[2,256,1792]{2,1,0:T(8,128)S(1)} %get-tuple-element.7.total), custom_call_target="tpu_custom_call" | custom-call | tf_op jit(solution)/shard_map/pallas_call | solution.py:601
